TPU v7x, 32 devices: a whole 2x2x4 slice. The times are simulated.
32 devices in a mesh: dom: 16 (over z, y, x), grp: 2 (over core).
Axes of the slice: x: 2, y: 2, z: 4, core: 2. Of those that a mesh axis runs over, the one named last changes fastest.
Arguments:
- tangent_tiles: bfloat16 [4096, 128, 128], P(('grp', 'dom')), parts along dimension 0, may hold values from -0.5 to 0.5
- tile_blocks: int32 [2048, 2], P('dom'), may hold values from 0 to 127, as said below
- block_home: int32 [128], replicated, may hold values from 0 to 127, as said below
- tile_count: int32 [16], P('dom'), may hold values from 48 to 128, as said below
- basis: bfloat16 [16384, 256], P('dom'), may hold values from -0.29882812 to 0.29882812
Outputs:
- reduced: float32 [512, 256], P('grp'), parts along dimension 0
There are 2 independent parts, one for each index of `grp`. A program takes and returns all parts, laid end to end along the dimension named above; an argument that names none is the same for every part. Nothing has to cross between parts.
Inputs may be any that keep to these rules, and one draw needn't show every extreme that they name: `tile_blocks`: every row block named by a device's tile slots has its position held by one of the devices with dom index from that device's index - 4 to its index + 8 // 2 - 1, taken cyclically. Among the row blocks named by one device's 128 slots, at most 2 distinct ones have their position held by any one device; every device reaches 2 for some holder. `block_home`: A permutation of the row blocks. `tile_count`: some device has exactly 128 live slots.
All inputs are finite; a program needn't handle non-finite values.
Results may differ from a plain program's by a relative error of at most 0.0029.
Values may be sent and summed in bfloat16 or wider, within the bound.
A program may use at most 64 MiB of HBM per device.

v0:
```python
import jax
import jax.numpy as jnp
from jax import lax
from jax.sharding import PartitionSpec as P

CAP = 2
NEAR = 8
GROUP = 16


def shifted(value, axis, steps):
    count = lax.axis_size(axis)
    pairs = [(source, (source + steps) % count) for source in range(count)]
    return lax.ppermute(value, axis, pairs)


def on_device(tangent_tiles, tile_blocks, block_home, tile_count, basis):
    ndom = lax.axis_size("dom")
    tile_dev = tangent_tiles.shape[0]
    block = tangent_tiles.shape[1]
    rank = basis.shape[1]
    blk_dev = basis.shape[0] // block
    stored = basis.reshape(blk_dev, block, rank)
    place = jnp.take(block_home, tile_blocks.reshape(-1), axis=0)
    places = jnp.arange(ndom * blk_dev, dtype=jnp.int32)
    wanted = jnp.any(place[:, None] == places[None, :], axis=0).astype(jnp.int32)
    wanted = wanted.reshape(ndom, blk_dev)
    order = jnp.cumsum(wanted, axis=1) - 1
    levels = jnp.arange(CAP, dtype=jnp.int32)
    chosen = (wanted[:, :, None] == 1) & (order[:, :, None] == levels[None, None, :])
    local_ids = jnp.arange(blk_dev, dtype=jnp.int32)[None, :, None]
    requests = jnp.sum(jnp.where(chosen, local_ids, 0), axis=1)
    holder = place // blk_dev
    flat_order = order.reshape(-1)
    level_of = jnp.take(flat_order, place, axis=0)
    myself = lax.axis_index("dom")
    pieces = []
    for step_k in range(NEAR):
        away = step_k - NEAR // 2
        target = (myself + away) % ndom
        asking = lax.dynamic_index_in_dim(requests, target, 0, keepdims=False)
        if away == 0:
            pieces.append(jnp.take(stored, asking, axis=0))
        else:
            asked = shifted(asking, "dom", away)
            served = jnp.take(stored, asked, axis=0)
            pieces.append(shifted(served, "dom", -away))
    fetched = jnp.concatenate(pieces, axis=0)
    window_pos = (holder - myself + NEAR // 2) % ndom
    slot_of = window_pos * CAP + level_of
    slot_of = slot_of.reshape(tile_dev, 2)
    live = (jnp.arange(tile_dev, dtype=jnp.int32) < tile_count[0]).astype(jnp.float32)

    def project(step, total):
        begin = step * GROUP
        tile_set = lax.dynamic_slice_in_dim(tangent_tiles, begin, GROUP, 0)
        link_set = lax.dynamic_slice_in_dim(slot_of, begin, GROUP, 0)
        live_set = lax.dynamic_slice_in_dim(live, begin, GROUP, 0)
        cols = jnp.take(fetched, link_set[:, 1], axis=0)
        rows = jnp.take(fetched, link_set[:, 0], axis=0)
        right = jnp.einsum("tab,tbr->tar", tile_set, cols, preferred_element_type=jnp.float32)
        right = (right * live_set[:, None, None]).astype(jnp.bfloat16)
        return total + jnp.einsum(
            "ar,as->rs",
            rows.reshape(GROUP * block, rank),
            right.reshape(GROUP * block, rank),
            preferred_element_type=jnp.float32,
        )

    partial_sum = lax.fori_loop(0, tile_dev // GROUP, project, jnp.zeros((rank, rank), jnp.float32))
    reduced = lax.psum(partial_sum, "dom")
    return reduced


def solution(mesh):
    return jax.shard_map(
        on_device,
        mesh=mesh,
        in_specs=(P(("grp", "dom"), None, None), P("dom", None), P(), P("dom"), P("dom", None)),
        out_specs=P("grp", None),
        check_vma=False,
    )
```

profile of v0, /device:TPU:0, one launch (start us, length us, event | category | flops | bytes accessed | tf_op | source)
XLA Modules:
  0.0 211.4 jit_solution(7998382532682025767)
XLA Ops:
  7.5 1.9 gather_fusion.2
  10.3 4.0 %collective-permute-start.12 = (s32[2]{0:T(128)S(1)}, s32[2]{0:T(128)S(1)}, u32[]{:S(2)}, u32[]{:S(2)}) collective-permute-start(s32[2]{0:T(128)S(1)} %get-tuple-element.157), channel_id=1, source_target_pairs={{0,6},{2,8},{4,10},{6,12},{8,14},{10,16},{12,18},{14,20},{16,22},{... | collective-permute-start | bytes 32 | tf_op jit(solution)/shard_map/ppermute | solution.py:14
  14.3 1.5 collective-permute-start.10
  16.4 5.0 %collective-permute-start.6 = (s32[2]{0:T(128)S(1)}, s32[2]{0:T(128)S(1)}, u32[]{:S(2)}, u32[]{:S(2)}) collective-permute-start(s32[2]{0:T(128)S(1)} %get-tuple-element.161), channel_id=1, source_target_pairs={{0,30},{2,0},{4,2},{6,4},{8,6},{10,8},{12,10},{14,12},{16,14},{18,... | collective-permute-start | bytes 32 | tf_op jit(solution)/shard_map/ppermute | solution.py:14
  22.8 1.9 gather_fusion.3
  25.9 1.5 collective-permute-start
  27.5 2.5 %collective-permute-done.2 = s32[2]{0:T(128)S(1)} collective-permute-done((s32[2]{0:T(128)S(1)}, s32[2]{0:T(128)S(1)}, u32[]{:S(2)}, u32[]{:S(2)}) %collective-permute-start.2) | collective-permute-done | bytes 40 | tf_op jit(solution)/shard_map/ppermute | solution.py:14
  34.1 5.0 %collective-permute-start.13 = (bf16[2,128,256]{2,1,0:T(8,128)(2,1)S(1)}, bf16[2,128,256]{2,1,0:T(8,128)(2,1)S(1)}, u32[]{:S(2)}, u32[]{:S(2)}) collective-permute-start(bf16[2,128,256]{2,1,0:T(8,128)(2,1)S(1)} %broadcast_select_fusion), channel_id=1, source_target_pairs={{0,26},{2,28},{4,30},{6,0},{8,2},{10,4},{12,6},{14,8},{16,10},{18,... | collective-permute-start | bytes 393224 | tf_op jit(solution)/shard_map/ppermute | solution.py:14
  39.4 1.5 collective-permute-start.9
  41.0 2.0 collective-permute-start.3
  43.4 6.5 %collective-permute-done.1 = bf16[2,128,256]{2,1,0:T(8,128)(2,1)S(1)} collective-permute-done((bf16[2,128,256]{2,1,0:T(8,128)(2,1)S(1)}, bf16[2,128,256]{2,1,0:T(8,128)(2,1)S(1)}, u32[]{:S(2)}, u32[]{:S(2)}) %collective-permute-start.1) | collective-permute-done | bytes 131104 | tf_op jit(solution)/shard_map/ppermute | solution.py:14
  51.6 6.0 %collective-permute-done.5 = bf16[2,128,256]{2,1,0:T(8,128)(2,1)S(1)} collective-permute-done((bf16[2,128,256]{2,1,0:T(8,128)(2,1)S(1)}, bf16[2,128,256]{2,1,0:T(8,128)(2,1)S(1)}, u32[]{:S(2)}, u32[]{:S(2)}) %collective-permute-start.5) | collective-permute-done | bytes 131104 | tf_op jit(solution)/shard_map/ppermute | solution.py:14
  57.6 2.5 %collective-permute-done.7 = bf16[2,128,256]{2,1,0:T(8,128)(2,1)S(1)} collective-permute-done((bf16[2,128,256]{2,1,0:T(8,128)(2,1)S(1)}, bf16[2,128,256]{2,1,0:T(8,128)(2,1)S(1)}, u32[]{:S(2)}, u32[]{:S(2)}) %collective-permute-start.7) | collective-permute-done | bytes 131104 | tf_op jit(solution)/shard_map/ppermute | solution.py:14
  60.3 37.5 %while.14 = (s32[]{:T(128)}, f32[256,256]{1,0:T(8,128)S(1)}, s32[128,2]{0,1:T(2,128)S(1)}, bf16[16,128,256]{2,1,0:T(8,128)(2,1)S(1)}, bf16[128,128,128]{2,1,0:T(...) while((s32[]{:T(128)}, f32[256,256]{1,0:T(8,128)S(1)}, ...), condition=%wide.region_4.8_spmd.clone, body=%wide.region_3.7_spmd.clone.sunk | while | flops 404883648 | bytes 7349425 | solution.py:70
  61.1 1.6 gather_fusion.1
  62.7 2.3 %fusion.38 = f32[256,256]{1,0:T(8,128)S(1)} fusion(bf16[16,128,256]{2,1,0:T(8,128)(2,1)S(1)} %gather_fusion, bf16[16,128,256]{2,1,0:T(8,128)(2,1)} %gather_fusion.1, f32[16]{0:T(128)S(1)} %dynamic_slice.90, pred[16]{0:T(512)(128)(4,1)S(1)} %get-tuple-element.246, pred[16]{0:T(512)(128)(4,1)S(1)} %get-tuple-element.247, ...), kind=kOutput, calls=%fused_computation.15.clone.1 | convolution fusion | flops 404881408 | bytes 3145829 | tf_op jit(solution)/shard_map/while/body/eval_jaxpr/ar,as->rs/dot_general | solution.py:63
  65.8 1.6 gather_fusion.1
  67.4 2.3 %fusion.38 = f32[256,256]{1,0:T(8,128)S(1)} fusion(bf16[16,128,256]{2,1,0:T(8,128)(2,1)S(1)} %gather_fusion, bf16[16,128,256]{2,1,0:T(8,128)(2,1)} %gather_fusion.1, f32[16]{0:T(128)S(1)} %dynamic_slice.90, pred[16]{0:T(512)(128)(4,1)S(1)} %get-tuple-element.246, pred[16]{0:T(512)(128)(4,1)S(1)} %get-tuple-element.247, ...), kind=kOutput, calls=%fused_computation.15.clone.1 | convolution fusion | flops 404881408 | bytes 3145829 | tf_op jit(solution)/shard_map/while/body/eval_jaxpr/ar,as->rs/dot_general | solution.py:63
  70.5 1.6 gather_fusion.1
  72.1 2.3 %fusion.38 = f32[256,256]{1,0:T(8,128)S(1)} fusion(bf16[16,128,256]{2,1,0:T(8,128)(2,1)S(1)} %gather_fusion, bf16[16,128,256]{2,1,0:T(8,128)(2,1)} %gather_fusion.1, f32[16]{0:T(128)S(1)} %dynamic_slice.90, pred[16]{0:T(512)(128)(4,1)S(1)} %get-tuple-element.246, pred[16]{0:T(512)(128)(4,1)S(1)} %get-tuple-element.247, ...), kind=kOutput, calls=%fused_computation.15.clone.1 | convolution fusion | flops 404881408 | bytes 3145829 | tf_op jit(solution)/shard_map/while/body/eval_jaxpr/ar,as->rs/dot_general | solution.py:63
  75.2 1.6 gather_fusion.1
  76.8 2.3 %fusion.38 = f32[256,256]{1,0:T(8,128)S(1)} fusion(bf16[16,128,256]{2,1,0:T(8,128)(2,1)S(1)} %gather_fusion, bf16[16,128,256]{2,1,0:T(8,128)(2,1)} %gather_fusion.1, f32[16]{0:T(128)S(1)} %dynamic_slice.90, pred[16]{0:T(512)(128)(4,1)S(1)} %get-tuple-element.246, pred[16]{0:T(512)(128)(4,1)S(1)} %get-tuple-element.247, ...), kind=kOutput, calls=%fused_computation.15.clone.1 | convolution fusion | flops 404881408 | bytes 3145829 | tf_op jit(solution)/shard_map/while/body/eval_jaxpr/ar,as->rs/dot_general | solution.py:63
  79.9 1.6 gather_fusion.1
  81.5 2.3 %fusion.38 = f32[256,256]{1,0:T(8,128)S(1)} fusion(bf16[16,128,256]{2,1,0:T(8,128)(2,1)S(1)} %gather_fusion, bf16[16,128,256]{2,1,0:T(8,128)(2,1)} %gather_fusion.1, f32[16]{0:T(128)S(1)} %dynamic_slice.90, pred[16]{0:T(512)(128)(4,1)S(1)} %get-tuple-element.246, pred[16]{0:T(512)(128)(4,1)S(1)} %get-tuple-element.247, ...), kind=kOutput, calls=%fused_computation.15.clone.1 | convolution fusion | flops 404881408 | bytes 3145829 | tf_op jit(solution)/shard_map/while/body/eval_jaxpr/ar,as->rs/dot_general | solution.py:63
  84.5 1.6 gather_fusion.1
  86.2 2.3 %fusion.38 = f32[256,256]{1,0:T(8,128)S(1)} fusion(bf16[16,128,256]{2,1,0:T(8,128)(2,1)S(1)} %gather_fusion, bf16[16,128,256]{2,1,0:T(8,128)(2,1)} %gather_fusion.1, f32[16]{0:T(128)S(1)} %dynamic_slice.90, pred[16]{0:T(512)(128)(4,1)S(1)} %get-tuple-element.246, pred[16]{0:T(512)(128)(4,1)S(1)} %get-tuple-element.247, ...), kind=kOutput, calls=%fused_computation.15.clone.1 | convolution fusion | flops 404881408 | bytes 3145829 | tf_op jit(solution)/shard_map/while/body/eval_jaxpr/ar,as->rs/dot_general | solution.py:63
  89.2 1.6 gather_fusion.1
  90.8 2.3 %fusion.38 = f32[256,256]{1,0:T(8,128)S(1)} fusion(bf16[16,128,256]{2,1,0:T(8,128)(2,1)S(1)} %gather_fusion, bf16[16,128,256]{2,1,0:T(8,128)(2,1)} %gather_fusion.1, f32[16]{0:T(128)S(1)} %dynamic_slice.90, pred[16]{0:T(512)(128)(4,1)S(1)} %get-tuple-element.246, pred[16]{0:T(512)(128)(4,1)S(1)} %get-tuple-element.247, ...), kind=kOutput, calls=%fused_computation.15.clone.1 | convolution fusion | flops 404881408 | bytes 3145829 | tf_op jit(solution)/shard_map/while/body/eval_jaxpr/ar,as->rs/dot_general | solution.py:63
  93.9 1.6 gather_fusion.1
  95.5 2.3 %fusion.38 = f32[256,256]{1,0:T(8,128)S(1)} fusion(bf16[16,128,256]{2,1,0:T(8,128)(2,1)S(1)} %gather_fusion, bf16[16,128,256]{2,1,0:T(8,128)(2,1)} %gather_fusion.1, f32[16]{0:T(128)S(1)} %dynamic_slice.90, pred[16]{0:T(512)(128)(4,1)S(1)} %get-tuple-element.246, pred[16]{0:T(512)(128)(4,1)S(1)} %get-tuple-element.247, ...), kind=kOutput, calls=%fused_computation.15.clone.1 | convolution fusion | flops 404881408 | bytes 3145829 | tf_op jit(solution)/shard_map/while/body/eval_jaxpr/ar,as->rs/dot_general | solution.py:63
  98.5 104.3 %all-reduce.2.cloned.1.call-done = f32[256,256]{1,0:T(8,128)} async-done(((f32[256,256]{1,0:T(8,128)}), f32[256,256]{1,0:T(8,128)}) %all-reduce.2.cloned.1.call-update) | async-done | bytes 262160 | tf_op jit(solution)/shard_map/psum | solution.py:71
  202.9 1.7 copy.36
  (126 shorter events, 17.7 us)
Async XLA Ops:
  6.5 18.3 %copy-start = (bf16[1024,256]{1,0:T(8,128)(2,1)S(1)}, bf16[1024,256]{1,0:T(8,128)(2,1)}, u32[]{:S(2)}) copy-start(bf16[1024,256]{1,0:T(8,128)(2,1)} %param.17) | copy-start | bytes 1572868
  6.5 196.3 %all-reduce.2.cloned.1.call-start = ((), (), s32[]{:S(2)}) async-start(), calls=%async_computation | async-start | bytes 524288 | tf_op jit(solution)/shard_map/psum | solution.py:71
  10.3 15.1 %collective-permute-start.12 = (s32[2]{0:T(128)S(1)}, s32[2]{0:T(128)S(1)}, u32[]{:S(2)}, u32[]{:S(2)}) collective-permute-start(s32[2]{0:T(128)S(1)} %get-tuple-element.157), channel_id=1, source_target_pairs={{0,6},{2,8},{4,10},{6,12},{8,14},{10,16},{12,18},{14,20},{16,22},{... | collective-permute-start | bytes 32 | tf_op jit(solution)/shard_map/ppermute | solution.py:14
  14.3 11.6 %collective-permute-start.10 = (s32[2]{0:T(128)S(1)}, s32[2]{0:T(128)S(1)}, u32[]{:S(2)}, u32[]{:S(2)}) collective-permute-start(s32[2]{0:T(128)S(1)} %get-tuple-element.158), channel_id=1, source_target_pairs={{0,4},{2,6},{4,8},{6,10},{8,12},{10,14},{12,16},{14,18},{16,20},{1... | collective-permute-start | bytes 32 | tf_op jit(solution)/shard_map/ppermute | solution.py:14
  15.8 11.6 %collective-permute-start.8 = (s32[2]{0:T(128)S(1)}, s32[2]{0:T(128)S(1)}, u32[]{:S(2)}, u32[]{:S(2)}) collective-permute-start(s32[2]{0:T(128)S(1)} %get-tuple-element.159), channel_id=1, source_target_pairs={{0,2},{2,4},{4,6},{6,8},{8,10},{10,12},{12,14},{14,16},{16,18},{18... | collective-permute-start | bytes 32 | tf_op jit(solution)/shard_map/ppermute | solution.py:14
  16.4 11.0 %collective-permute-start.6 = (s32[2]{0:T(128)S(1)}, s32[2]{0:T(128)S(1)}, u32[]{:S(2)}, u32[]{:S(2)}) collective-permute-start(s32[2]{0:T(128)S(1)} %get-tuple-element.161), channel_id=1, source_target_pairs={{0,30},{2,0},{4,2},{6,4},{8,6},{10,8},{12,10},{14,12},{16,14},{18,... | collective-permute-start | bytes 32 | tf_op jit(solution)/shard_map/ppermute | solution.py:14
  21.5 6.0 %collective-permute-start.4 = (s32[2]{0:T(128)S(1)}, s32[2]{0:T(128)S(1)}, u32[]{:S(2)}, u32[]{:S(2)}) collective-permute-start(s32[2]{0:T(128)S(1)} %get-tuple-element.162), channel_id=1, source_target_pairs={{0,28},{2,30},{4,0},{6,2},{8,4},{10,6},{12,8},{14,10},{16,12},{18,... | collective-permute-start | bytes 32 | tf_op jit(solution)/shard_map/ppermute | solution.py:14
  25.5 4.5 %collective-permute-start.2 = (s32[2]{0:T(128)S(1)}, s32[2]{0:T(128)S(1)}, u32[]{:S(2)}, u32[]{:S(2)}) collective-permute-start(s32[2]{0:T(128)S(1)} %get-tuple-element.163), channel_id=1, source_target_pairs={{0,26},{2,28},{4,30},{6,0},{8,2},{10,4},{12,6},{14,8},{16,10},{18,... | collective-permute-start | bytes 32 | tf_op jit(solution)/shard_map/ppermute | solution.py:14
  25.9 4.2 %collective-permute-start = (s32[2]{0:T(128)S(1)}, s32[2]{0:T(128)S(1)}, u32[]{:S(2)}, u32[]{:S(2)}) collective-permute-start(s32[2]{0:T(128)S(1)} %get-tuple-element.164), channel_id=1, source_target_pairs={{0,24},{2,26},{4,28},{6,30},{8,0},{10,2},{12,4},{14,6},{16,8},{18,... | collective-permute-start | bytes 32 | tf_op jit(solution)/shard_map/ppermute | solution.py:14
  34.1 26.2 %collective-permute-start.13 = (bf16[2,128,256]{2,1,0:T(8,128)(2,1)S(1)}, bf16[2,128,256]{2,1,0:T(8,128)(2,1)S(1)}, u32[]{:S(2)}, u32[]{:S(2)}) collective-permute-start(bf16[2,128,256]{2,1,0:T(8,128)(2,1)S(1)} %broadcast_select_fusion), channel_id=1, source_target_pairs={{0,26},{2,28},{4,30},{6,0},{8,2},{10,4},{12,6},{14,8},{16,10},{18,... | collective-permute-start | bytes 393224 | tf_op jit(solution)/shard_map/ppermute | solution.py:14
  39.2 21.1 %collective-permute-start.11 = (bf16[2,128,256]{2,1,0:T(8,128)(2,1)S(1)}, bf16[2,128,256]{2,1,0:T(8,128)(2,1)S(1)}, u32[]{:S(2)}, u32[]{:S(2)}) collective-permute-start(bf16[2,128,256]{2,1,0:T(8,128)(2,1)S(1)} %broadcast_select_fusion.1), channel_id=1, source_target_pairs={{0,28},{2,30},{4,0},{6,2},{8,4},{10,6},{12,8},{14,10},{16,12},{18,... | collective-permute-start | bytes 393224 | tf_op jit(solution)/shard_map/ppermute | solution.py:14
  39.4 20.9 %collective-permute-start.9 = (bf16[2,128,256]{2,1,0:T(8,128)(2,1)S(1)}, bf16[2,128,256]{2,1,0:T(8,128)(2,1)S(1)}, u32[]{:S(2)}, u32[]{:S(2)}) collective-permute-start(bf16[2,128,256]{2,1,0:T(8,128)(2,1)S(1)} %broadcast_select_fusion.2), channel_id=1, source_target_pairs={{0,30},{2,0},{4,2},{6,4},{8,6},{10,8},{12,10},{14,12},{16,14},{18,... | collective-permute-start | bytes 393224 | tf_op jit(solution)/shard_map/ppermute | solution.py:14
  41.0 10.5 %collective-permute-start.3 = (bf16[2,128,256]{2,1,0:T(8,128)(2,1)S(1)}, bf16[2,128,256]{2,1,0:T(8,128)(2,1)S(1)}, u32[]{:S(2)}, u32[]{:S(2)}) collective-permute-start(bf16[2,128,256]{2,1,0:T(8,128)(2,1)S(1)} %broadcast_select_fusion.5), channel_id=1, source_target_pairs={{0,6},{2,8},{4,10},{6,12},{8,14},{10,16},{12,18},{14,20},{16,22},{... | collective-permute-start | bytes 393224 | tf_op jit(solution)/shard_map/ppermute | solution.py:14
  43.1 6.8 %collective-permute-start.1 = (bf16[2,128,256]{2,1,0:T(8,128)(2,1)S(1)}, bf16[2,128,256]{2,1,0:T(8,128)(2,1)S(1)}, u32[]{:S(2)}, u32[]{:S(2)}) collective-permute-start(bf16[2,128,256]{2,1,0:T(8,128)(2,1)S(1)} %broadcast_select_fusion.6), channel_id=1, source_target_pairs={{0,8},{2,10},{4,12},{6,14},{8,16},{10,18},{12,20},{14,22},{16,24},... | collective-permute-start | bytes 393224 | tf_op jit(solution)/shard_map/ppermute | solution.py:14
  49.9 7.7 %collective-permute-start.5 = (bf16[2,128,256]{2,1,0:T(8,128)(2,1)S(1)}, bf16[2,128,256]{2,1,0:T(8,128)(2,1)S(1)}, u32[]{:S(2)}, u32[]{:S(2)}) collective-permute-start(bf16[2,128,256]{2,1,0:T(8,128)(2,1)S(1)} %broadcast_select_fusion.4), channel_id=1, source_target_pairs={{0,4},{2,6},{4,8},{6,10},{8,12},{10,14},{12,16},{14,18},{16,20},{1... | collective-permute-start | bytes 393224 | tf_op jit(solution)/shard_map/ppermute | solution.py:14
  51.5 8.6 %collective-permute-start.7 = (bf16[2,128,256]{2,1,0:T(8,128)(2,1)S(1)}, bf16[2,128,256]{2,1,0:T(8,128)(2,1)S(1)}, u32[]{:S(2)}, u32[]{:S(2)}) collective-permute-start(bf16[2,128,256]{2,1,0:T(8,128)(2,1)S(1)} %broadcast_select_fusion.3), channel_id=1, source_target_pairs={{0,2},{2,4},{4,6},{6,8},{8,10},{10,12},{12,14},{14,16},{16,18},{18... | collective-permute-start | bytes 393224 | tf_op jit(solution)/shard_map/ppermute | solution.py:14
  97.8 0.7 copy-start.1
Sparse Core Ops, SparseCore 0:
  98.6 104.1 all-reduce.1
where the time goes:
time: 212 us; the launch traced here: 211 us
  waiting for transfers between devices  122 us (58%)
  local copies, waits for them, and re-layouts  31.4 us (15%)
  starting transfers between devices  23.9 us (11%)
  matrix products  18 us (8%)
  between operations  14.5 us (7%)
    psum x1, waiting for transfers between devices, on_device(): reduced = lax.psum(partial_sum, 'dom')  104 us
    ppermute x14, starting transfers between devices, shifted(): return lax.ppermute(value, axis, pairs)  23.9 us
    dot_general x8, matrix products, project(): jnp.einsum('ar,as->rs', rows.reshape(GROUP * block, rank), right.reshape(...  18 us
    ppermute x14, waiting for transfers between devices, shifted(): return lax.ppermute(value, axis, pairs)  17.6 us
    gather x8, local copies, waits for them, and re-layouts, project(): rows = jnp.take(fetched, link_set[:, 0], axis=0)  12.8 us
    gather x8, local copies, waits for them, and re-layouts, project(): cols = jnp.take(fetched, link_set[:, 1], axis=0)  4.91 us
  transfers between devices with their start and end apart: 15, of which 5 were waited for; matrix products, arithmetic and copies ran while one was open for 2% of the time, Pallas kernels for 0%

commit v1 on v0

--- a/solution.py
+++ b/solution.py
@@ -68,7 +68,7 @@
         )
 
     partial_sum = lax.fori_loop(0, tile_dev // GROUP, project, jnp.zeros((rank, rank), jnp.float32))
-    reduced = lax.psum(partial_sum, "dom")
+    reduced = jnp.sum(lax.all_gather(partial_sum, "dom"), axis=0)
     return reduced
 
 

time: 212 us -> 181 us (0.85)
  waiting for transfers between devices: 122 us -> 89.6 us
  other arithmetic: 1.3 us -> 4.48 us
    psum x1 -> x0, waiting for transfers between devices: 104 us -> none  [on_device(): reduced = lax.psum(partial_sum, 'dom')]
    all_gather x0 -> x1, waiting for transfers between devices: none -> 72.1 us  [on_device(): reduced = jnp.sum(lax.all_gather(partial_sum, 'dom'), axis=0)]
    reduce_sum x0 -> x1, other arithmetic: none -> 3.18 us  [on_device(): reduced = jnp.sum(lax.all_gather(partial_sum, 'dom'), axis=0)]
where the time goes in v1:
time: 181 us
  waiting for transfers between devices  89.6 us (50%)
  local copies, waits for them, and re-layouts  29.7 us (16%)
  starting transfers between devices  23.9 us (13%)
  matrix products  18 us (10%)
  between operations  14.5 us (8%)
  other arithmetic  4.48 us (2%)
    all_gather x1, waiting for transfers between devices, on_device(): reduced = jnp.sum(lax.all_gather(partial_sum, 'dom'), axis=0)  72.1 us
    ppermute x14, starting transfers between devices, shifted(): return lax.ppermute(value, axis, pairs)  23.9 us
    dot_general x8, matrix products, project(): jnp.einsum('ar,as->rs', rows.reshape(GROUP * block, rank), right.reshape(...  18 us
    ppermute x14, waiting for transfers between devices, shifted(): return lax.ppermute(value, axis, pairs)  17.6 us
    gather x8, local copies, waits for them, and re-layouts, project(): rows = jnp.take(fetched, link_set[:, 0], axis=0)  12.8 us
    gather x8, local copies, waits for them, and re-layouts, project(): cols = jnp.take(fetched, link_set[:, 1], axis=0)  4.91 us
    gather x7, local copies, waits for them, and re-layouts, on_device(): served = jnp.take(stored, asked, axis=0)  3.89 us
  transfers between devices with their start and end apart: 15, of which 5 were waited for; matrix products, arithmetic and copies ran while one was open for 2% of the time, Pallas kernels for 0%

profile of v1, /device:TPU:0, one launch (start us, length us, event | category | flops | bytes accessed | tf_op | source)
XLA Modules:
  0.0 180.6 jit_solution(5840417314438624343)
XLA Ops:
  7.5 1.9 %gather_fusion.2 = s32[256]{0:T(256)S(1)} fusion(s32[128]{0:T(128)} %param.15, s32[1024]{0:T(1024)S(1)} %pad_clamp_fusion.11), kind=kCustom, calls=%fused_computation.clone | custom fusion | bytes 3072 | tf_op jit(solution)/shard_map/jit(_take)/gather | solution.py:24
  10.3 4.0 %collective-permute-start.12 = (s32[2]{0:T(128)S(1)}, s32[2]{0:T(128)S(1)}, u32[]{:S(2)}, u32[]{:S(2)}) collective-permute-start(s32[2]{0:T(128)S(1)} %get-tuple-element.157), channel_id=1, source_target_pairs={{0,6},{2,8},{4,10},{6,12},{8,14},{10,16},{12,18},{14,20},{16,22},{... | collective-permute-start | bytes 32 | tf_op jit(solution)/shard_map/ppermute | solution.py:14
  14.3 1.5 collective-permute-start.10
  16.4 5.0 %collective-permute-start.6 = (s32[2]{0:T(128)S(1)}, s32[2]{0:T(128)S(1)}, u32[]{:S(2)}, u32[]{:S(2)}) collective-permute-start(s32[2]{0:T(128)S(1)} %get-tuple-element.161), channel_id=1, source_target_pairs={{0,30},{2,0},{4,2},{6,4},{8,6},{10,8},{12,10},{14,12},{16,14},{18,... | collective-permute-start | bytes 32 | tf_op jit(solution)/shard_map/ppermute | solution.py:14
  22.8 1.9 %gather_fusion.3 = s32[256]{0:T(256)S(1)} fusion(s32[128]{0:T(128)S(1)} %sub.22, s32[1024]{0:T(1024)S(1)} %pad_clamp_fusion.10), kind=kCustom, calls=%fused_computation.3.clone | custom fusion | bytes 3072 | tf_op jit(solution)/shard_map/jit(_take)/gather | solution.py:35
  25.9 1.5 collective-permute-start
  27.5 2.5 %collective-permute-done.2 = s32[2]{0:T(128)S(1)} collective-permute-done((s32[2]{0:T(128)S(1)}, s32[2]{0:T(128)S(1)}, u32[]{:S(2)}, u32[]{:S(2)}) %collective-permute-start.2) | collective-permute-done | bytes 40 | tf_op jit(solution)/shard_map/ppermute | solution.py:14
  34.1 5.0 %collective-permute-start.13 = (bf16[2,128,256]{2,1,0:T(8,128)(2,1)S(1)}, bf16[2,128,256]{2,1,0:T(8,128)(2,1)S(1)}, u32[]{:S(2)}, u32[]{:S(2)}) collective-permute-start(bf16[2,128,256]{2,1,0:T(8,128)(2,1)S(1)} %broadcast_select_fusion), channel_id=1, source_target_pairs={{0,26},{2,28},{4,30},{6,0},{8,2},{10,4},{12,6},{14,8},{16,10},{18,... | collective-permute-start | bytes 393224 | tf_op jit(solution)/shard_map/ppermute | solution.py:14
  39.4 1.5 collective-permute-start.9
  41.0 2.0 %collective-permute-start.3 = (bf16[2,128,256]{2,1,0:T(8,128)(2,1)S(1)}, bf16[2,128,256]{2,1,0:T(8,128)(2,1)S(1)}, u32[]{:S(2)}, u32[]{:S(2)}) collective-permute-start(bf16[2,128,256]{2,1,0:T(8,128)(2,1)S(1)} %broadcast_select_fusion.5), channel_id=1, source_target_pairs={{0,6},{2,8},{4,10},{6,12},{8,14},{10,16},{12,18},{14,20},{16,22},{... | collective-permute-start | bytes 393224 | tf_op jit(solution)/shard_map/ppermute | solution.py:14
  43.4 6.5 %collective-permute-done.1 = bf16[2,128,256]{2,1,0:T(8,128)(2,1)S(1)} collective-permute-done((bf16[2,128,256]{2,1,0:T(8,128)(2,1)S(1)}, bf16[2,128,256]{2,1,0:T(8,128)(2,1)S(1)}, u32[]{:S(2)}, u32[]{:S(2)}) %collective-permute-start.1) | collective-permute-done | bytes 131104 | tf_op jit(solution)/shard_map/ppermute | solution.py:14
  51.6 6.0 %collective-permute-done.5 = bf16[2,128,256]{2,1,0:T(8,128)(2,1)S(1)} collective-permute-done((bf16[2,128,256]{2,1,0:T(8,128)(2,1)S(1)}, bf16[2,128,256]{2,1,0:T(8,128)(2,1)S(1)}, u32[]{:S(2)}, u32[]{:S(2)}) %collective-permute-start.5) | collective-permute-done | bytes 131104 | tf_op jit(solution)/shard_map/ppermute | solution.py:14
  57.6 2.5 %collective-permute-done.7 = bf16[2,128,256]{2,1,0:T(8,128)(2,1)S(1)} collective-permute-done((bf16[2,128,256]{2,1,0:T(8,128)(2,1)S(1)}, bf16[2,128,256]{2,1,0:T(8,128)(2,1)S(1)}, u32[]{:S(2)}, u32[]{:S(2)}) %collective-permute-start.7) | collective-permute-done | bytes 131104 | tf_op jit(solution)/shard_map/ppermute | solution.py:14
  60.3 37.5 %while.14 = (s32[]{:T(128)}, f32[256,256]{1,0:T(8,128)S(1)}, s32[128,2]{0,1:T(2,128)S(1)}, bf16[16,128,256]{2,1,0:T(8,128)(2,1)S(1)}, bf16[128,128,128]{2,1,0:T(...) while((s32[]{:T(128)}, f32[256,256]{1,0:T(8,128)S(1)}, ...), condition=%wide.region_4.8_spmd.clone, body=%wide.region_3.7_spmd.clone.sunk | while | flops 404883648 | bytes 7349425 | solution.py:70
  61.1 1.6 gather_fusion.1
  62.7 2.3 %fusion.38 = f32[256,256]{1,0:T(8,128)S(1)} fusion(bf16[16,128,256]{2,1,0:T(8,128)(2,1)S(1)} %gather_fusion, bf16[16,128,256]{2,1,0:T(8,128)(2,1)} %gather_fusion.1, f32[16]{0:T(128)S(1)} %dynamic_slice.90, pred[16]{0:T(512)(128)(4,1)S(1)} %get-tuple-element.246, pred[16]{0:T(512)(128)(4,1)S(1)} %get-tuple-element.247, ...), kind=kOutput, calls=%fused_computation.15.clone.1 | convolution fusion | flops 404881408 | bytes 3145829 | tf_op jit(solution)/shard_map/while/body/eval_jaxpr/ar,as->rs/dot_general | solution.py:63
  65.8 1.6 gather_fusion.1
  67.4 2.3 %fusion.38 = f32[256,256]{1,0:T(8,128)S(1)} fusion(bf16[16,128,256]{2,1,0:T(8,128)(2,1)S(1)} %gather_fusion, bf16[16,128,256]{2,1,0:T(8,128)(2,1)} %gather_fusion.1, f32[16]{0:T(128)S(1)} %dynamic_slice.90, pred[16]{0:T(512)(128)(4,1)S(1)} %get-tuple-element.246, pred[16]{0:T(512)(128)(4,1)S(1)} %get-tuple-element.247, ...), kind=kOutput, calls=%fused_computation.15.clone.1 | convolution fusion | flops 404881408 | bytes 3145829 | tf_op jit(solution)/shard_map/while/body/eval_jaxpr/ar,as->rs/dot_general | solution.py:63
  70.5 1.6 gather_fusion.1
  72.1 2.3 %fusion.38 = f32[256,256]{1,0:T(8,128)S(1)} fusion(bf16[16,128,256]{2,1,0:T(8,128)(2,1)S(1)} %gather_fusion, bf16[16,128,256]{2,1,0:T(8,128)(2,1)} %gather_fusion.1, f32[16]{0:T(128)S(1)} %dynamic_slice.90, pred[16]{0:T(512)(128)(4,1)S(1)} %get-tuple-element.246, pred[16]{0:T(512)(128)(4,1)S(1)} %get-tuple-element.247, ...), kind=kOutput, calls=%fused_computation.15.clone.1 | convolution fusion | flops 404881408 | bytes 3145829 | tf_op jit(solution)/shard_map/while/body/eval_jaxpr/ar,as->rs/dot_general | solution.py:63
  75.2 1.6 gather_fusion.1
  76.8 2.3 %fusion.38 = f32[256,256]{1,0:T(8,128)S(1)} fusion(bf16[16,128,256]{2,1,0:T(8,128)(2,1)S(1)} %gather_fusion, bf16[16,128,256]{2,1,0:T(8,128)(2,1)} %gather_fusion.1, f32[16]{0:T(128)S(1)} %dynamic_slice.90, pred[16]{0:T(512)(128)(4,1)S(1)} %get-tuple-element.246, pred[16]{0:T(512)(128)(4,1)S(1)} %get-tuple-element.247, ...), kind=kOutput, calls=%fused_computation.15.clone.1 | convolution fusion | flops 404881408 | bytes 3145829 | tf_op jit(solution)/shard_map/while/body/eval_jaxpr/ar,as->rs/dot_general | solution.py:63
  79.9 1.6 gather_fusion.1
  81.5 2.3 %fusion.38 = f32[256,256]{1,0:T(8,128)S(1)} fusion(bf16[16,128,256]{2,1,0:T(8,128)(2,1)S(1)} %gather_fusion, bf16[16,128,256]{2,1,0:T(8,128)(2,1)} %gather_fusion.1, f32[16]{0:T(128)S(1)} %dynamic_slice.90, pred[16]{0:T(512)(128)(4,1)S(1)} %get-tuple-element.246, pred[16]{0:T(512)(128)(4,1)S(1)} %get-tuple-element.247, ...), kind=kOutput, calls=%fused_computation.15.clone.1 | convolution fusion | flops 404881408 | bytes 3145829 | tf_op jit(solution)/shard_map/while/body/eval_jaxpr/ar,as->rs/dot_general | solution.py:63
  84.5 1.6 gather_fusion.1
  86.2 2.3 %fusion.38 = f32[256,256]{1,0:T(8,128)S(1)} fusion(bf16[16,128,256]{2,1,0:T(8,128)(2,1)S(1)} %gather_fusion, bf16[16,128,256]{2,1,0:T(8,128)(2,1)} %gather_fusion.1, f32[16]{0:T(128)S(1)} %dynamic_slice.90, pred[16]{0:T(512)(128)(4,1)S(1)} %get-tuple-element.246, pred[16]{0:T(512)(128)(4,1)S(1)} %get-tuple-element.247, ...), kind=kOutput, calls=%fused_computation.15.clone.1 | convolution fusion | flops 404881408 | bytes 3145829 | tf_op jit(solution)/shard_map/while/body/eval_jaxpr/ar,as->rs/dot_general | solution.py:63
  89.2 1.6 gather_fusion.1
  90.8 2.3 %fusion.38 = f32[256,256]{1,0:T(8,128)S(1)} fusion(bf16[16,128,256]{2,1,0:T(8,128)(2,1)S(1)} %gather_fusion, bf16[16,128,256]{2,1,0:T(8,128)(2,1)} %gather_fusion.1, f32[16]{0:T(128)S(1)} %dynamic_slice.90, pred[16]{0:T(512)(128)(4,1)S(1)} %get-tuple-element.246, pred[16]{0:T(512)(128)(4,1)S(1)} %get-tuple-element.247, ...), kind=kOutput, calls=%fused_computation.15.clone.1 | convolution fusion | flops 404881408 | bytes 3145829 | tf_op jit(solution)/shard_map/while/body/eval_jaxpr/ar,as->rs/dot_general | solution.py:63
  93.9 1.6 gather_fusion.1
  95.5 2.3 %fusion.38 = f32[256,256]{1,0:T(8,128)S(1)} fusion(bf16[16,128,256]{2,1,0:T(8,128)(2,1)S(1)} %gather_fusion, bf16[16,128,256]{2,1,0:T(8,128)(2,1)} %gather_fusion.1, f32[16]{0:T(128)S(1)} %dynamic_slice.90, pred[16]{0:T(512)(128)(4,1)S(1)} %get-tuple-element.246, pred[16]{0:T(512)(128)(4,1)S(1)} %get-tuple-element.247, ...), kind=kOutput, calls=%fused_computation.15.clone.1 | convolution fusion | flops 404881408 | bytes 3145829 | tf_op jit(solution)/shard_map/while/body/eval_jaxpr/ar,as->rs/dot_general | solution.py:63
  98.5 72.1 %all-gather.3.cloned.1.call-done = f32[4096,256]{1,0:T(8,128)} async-done(((f32[256,256]{1,0:T(8,128)}), f32[4096,256]{1,0:T(8,128)}) %all-gather.3.cloned.1.call-update) | async-done | bytes 4194320 | tf_op jit(solution)/shard_map/all_gather | solution.py:71
  170.6 3.2 %reduce_sum.19 = f32[256,256]{1,0:T(8,128)} reduce(f32[16,256,256]{2,1,0:T(8,128)} %bitcast.24, f32[]{:T(128)} %constant.157.clone.1), dimensions={0}, to_apply=%region_5.9 | reduce | flops 983040 | bytes 4456452 | tf_op jit(solution)/shard_map/reduce_sum | solution.py:71
  (126 shorter events, 17.7 us)
Async XLA Ops:
  6.5 18.3 %copy-start = (bf16[1024,256]{1,0:T(8,128)(2,1)S(1)}, bf16[1024,256]{1,0:T(8,128)(2,1)}, u32[]{:S(2)}) copy-start(bf16[1024,256]{1,0:T(8,128)(2,1)} %param.17) | copy-start | bytes 1572868
  6.5 164.0 %all-gather.3.cloned.1.call-start = ((), (), s32[]{:S(2)}) async-start(), calls=%async_computation | async-start | bytes 4456448 | tf_op jit(solution)/shard_map/all_gather | solution.py:71
  10.3 15.1 %collective-permute-start.12 = (s32[2]{0:T(128)S(1)}, s32[2]{0:T(128)S(1)}, u32[]{:S(2)}, u32[]{:S(2)}) collective-permute-start(s32[2]{0:T(128)S(1)} %get-tuple-element.157), channel_id=1, source_target_pairs={{0,6},{2,8},{4,10},{6,12},{8,14},{10,16},{12,18},{14,20},{16,22},{... | collective-permute-start | bytes 32 | tf_op jit(solution)/shard_map/ppermute | solution.py:14
  14.3 11.6 %collective-permute-start.10 = (s32[2]{0:T(128)S(1)}, s32[2]{0:T(128)S(1)}, u32[]{:S(2)}, u32[]{:S(2)}) collective-permute-start(s32[2]{0:T(128)S(1)} %get-tuple-element.158), channel_id=1, source_target_pairs={{0,4},{2,6},{4,8},{6,10},{8,12},{10,14},{12,16},{14,18},{16,20},{1... | collective-permute-start | bytes 32 | tf_op jit(solution)/shard_map/ppermute | solution.py:14
  15.8 11.6 %collective-permute-start.8 = (s32[2]{0:T(128)S(1)}, s32[2]{0:T(128)S(1)}, u32[]{:S(2)}, u32[]{:S(2)}) collective-permute-start(s32[2]{0:T(128)S(1)} %get-tuple-element.159), channel_id=1, source_target_pairs={{0,2},{2,4},{4,6},{6,8},{8,10},{10,12},{12,14},{14,16},{16,18},{18... | collective-permute-start | bytes 32 | tf_op jit(solution)/shard_map/ppermute | solution.py:14
  16.4 11.0 %collective-permute-start.6 = (s32[2]{0:T(128)S(1)}, s32[2]{0:T(128)S(1)}, u32[]{:S(2)}, u32[]{:S(2)}) collective-permute-start(s32[2]{0:T(128)S(1)} %get-tuple-element.161), channel_id=1, source_target_pairs={{0,30},{2,0},{4,2},{6,4},{8,6},{10,8},{12,10},{14,12},{16,14},{18,... | collective-permute-start | bytes 32 | tf_op jit(solution)/shard_map/ppermute | solution.py:14
  21.5 6.0 %collective-permute-start.4 = (s32[2]{0:T(128)S(1)}, s32[2]{0:T(128)S(1)}, u32[]{:S(2)}, u32[]{:S(2)}) collective-permute-start(s32[2]{0:T(128)S(1)} %get-tuple-element.162), channel_id=1, source_target_pairs={{0,28},{2,30},{4,0},{6,2},{8,4},{10,6},{12,8},{14,10},{16,12},{18,... | collective-permute-start | bytes 32 | tf_op jit(solution)/shard_map/ppermute | solution.py:14
  25.5 4.5 %collective-permute-start.2 = (s32[2]{0:T(128)S(1)}, s32[2]{0:T(128)S(1)}, u32[]{:S(2)}, u32[]{:S(2)}) collective-permute-start(s32[2]{0:T(128)S(1)} %get-tuple-element.163), channel_id=1, source_target_pairs={{0,26},{2,28},{4,30},{6,0},{8,2},{10,4},{12,6},{14,8},{16,10},{18,... | collective-permute-start | bytes 32 | tf_op jit(solution)/shard_map/ppermute | solution.py:14
  25.9 4.2 %collective-permute-start = (s32[2]{0:T(128)S(1)}, s32[2]{0:T(128)S(1)}, u32[]{:S(2)}, u32[]{:S(2)}) collective-permute-start(s32[2]{0:T(128)S(1)} %get-tuple-element.164), channel_id=1, source_target_pairs={{0,24},{2,26},{4,28},{6,30},{8,0},{10,2},{12,4},{14,6},{16,8},{18,... | collective-permute-start | bytes 32 | tf_op jit(solution)/shard_map/ppermute | solution.py:14
  34.1 26.2 %collective-permute-start.13 = (bf16[2,128,256]{2,1,0:T(8,128)(2,1)S(1)}, bf16[2,128,256]{2,1,0:T(8,128)(2,1)S(1)}, u32[]{:S(2)}, u32[]{:S(2)}) collective-permute-start(bf16[2,128,256]{2,1,0:T(8,128)(2,1)S(1)} %broadcast_select_fusion), channel_id=1, source_target_pairs={{0,26},{2,28},{4,30},{6,0},{8,2},{10,4},{12,6},{14,8},{16,10},{18,... | collective-permute-start | bytes 393224 | tf_op jit(solution)/shard_map/ppermute | solution.py:14
  39.2 21.1 %collective-permute-start.11 = (bf16[2,128,256]{2,1,0:T(8,128)(2,1)S(1)}, bf16[2,128,256]{2,1,0:T(8,128)(2,1)S(1)}, u32[]{:S(2)}, u32[]{:S(2)}) collective-permute-start(bf16[2,128,256]{2,1,0:T(8,128)(2,1)S(1)} %broadcast_select_fusion.1), channel_id=1, source_target_pairs={{0,28},{2,30},{4,0},{6,2},{8,4},{10,6},{12,8},{14,10},{16,12},{18,... | collective-permute-start | bytes 393224 | tf_op jit(solution)/shard_map/ppermute | solution.py:14
  39.4 20.9 %collective-permute-start.9 = (bf16[2,128,256]{2,1,0:T(8,128)(2,1)S(1)}, bf16[2,128,256]{2,1,0:T(8,128)(2,1)S(1)}, u32[]{:S(2)}, u32[]{:S(2)}) collective-permute-start(bf16[2,128,256]{2,1,0:T(8,128)(2,1)S(1)} %broadcast_select_fusion.2), channel_id=1, source_target_pairs={{0,30},{2,0},{4,2},{6,4},{8,6},{10,8},{12,10},{14,12},{16,14},{18,... | collective-permute-start | bytes 393224 | tf_op jit(solution)/shard_map/ppermute | solution.py:14
  41.0 10.5 %collective-permute-start.3 = (bf16[2,128,256]{2,1,0:T(8,128)(2,1)S(1)}, bf16[2,128,256]{2,1,0:T(8,128)(2,1)S(1)}, u32[]{:S(2)}, u32[]{:S(2)}) collective-permute-start(bf16[2,128,256]{2,1,0:T(8,128)(2,1)S(1)} %broadcast_select_fusion.5), channel_id=1, source_target_pairs={{0,6},{2,8},{4,10},{6,12},{8,14},{10,16},{12,18},{14,20},{16,22},{... | collective-permute-start | bytes 393224 | tf_op jit(solution)/shard_map/ppermute | solution.py:14
  43.1 6.8 %collective-permute-start.1 = (bf16[2,128,256]{2,1,0:T(8,128)(2,1)S(1)}, bf16[2,128,256]{2,1,0:T(8,128)(2,1)S(1)}, u32[]{:S(2)}, u32[]{:S(2)}) collective-permute-start(bf16[2,128,256]{2,1,0:T(8,128)(2,1)S(1)} %broadcast_select_fusion.6), channel_id=1, source_target_pairs={{0,8},{2,10},{4,12},{6,14},{8,16},{10,18},{12,20},{14,22},{16,24},... | collective-permute-start | bytes 393224 | tf_op jit(solution)/shard_map/ppermute | solution.py:14
  49.9 7.7 %collective-permute-start.5 = (bf16[2,128,256]{2,1,0:T(8,128)(2,1)S(1)}, bf16[2,128,256]{2,1,0:T(8,128)(2,1)S(1)}, u32[]{:S(2)}, u32[]{:S(2)}) collective-permute-start(bf16[2,128,256]{2,1,0:T(8,128)(2,1)S(1)} %broadcast_select_fusion.4), channel_id=1, source_target_pairs={{0,4},{2,6},{4,8},{6,10},{8,12},{10,14},{12,16},{14,18},{16,20},{1... | collective-permute-start | bytes 393224 | tf_op jit(solution)/shard_map/ppermute | solution.py:14
  51.5 8.6 %collective-permute-start.7 = (bf16[2,128,256]{2,1,0:T(8,128)(2,1)S(1)}, bf16[2,128,256]{2,1,0:T(8,128)(2,1)S(1)}, u32[]{:S(2)}, u32[]{:S(2)}) collective-permute-start(bf16[2,128,256]{2,1,0:T(8,128)(2,1)S(1)} %broadcast_select_fusion.3), channel_id=1, source_target_pairs={{0,2},{2,4},{4,6},{6,8},{8,10},{10,12},{12,14},{14,16},{16,18},{18... | collective-permute-start | bytes 393224 | tf_op jit(solution)/shard_map/ppermute | solution.py:14
  97.8 0.7 copy-start.1
Sparse Core Ops, SparseCore 0:
  98.6 71.8 all-gather.2
